TPU v7x, 8 devices: a whole 2x2x1 slice. The times are simulated.
8 devices in a mesh: seqs: 1 (over z), rows: 2 (over y), states: 4 (over x, core).
Axes of the slice: x: 2, y: 2, z: 1, core: 2. Of those that a mesh axis runs over, the one named last changes fastest.
Arguments:
- trans_mat: bfloat16 [4096, 2, 2048], P('rows', None, 'states')
- emit_mat: bfloat16 [4096, 50257], P(('rows', 'states'))
- init_dist: float32 [4096], P(('rows', 'states'))
- tokens: int32 [64, 4], P('seqs')
- lengths: int32 [64], P('seqs')
Outputs:
- output 1: float32 [64], P('seqs')
- output 2: float32 [64, 4096], P('seqs', ('rows', 'states'))
All inputs are finite; a program needn't handle non-finite values.
Results may differ from a plain program's by a relative error of at most 0.001.
Values are sent between devices in bfloat16 or wider.
A program may use at most 1 GiB of HBM per device.

v0:
```python
import jax
import jax.numpy as jnp
from jax import lax
from jax.sharding import PartitionSpec as P


def solution(mesh):
    vec_axes = ('rows', 'states')

    def local_forward(trans_blk, emit_blk, init_blk, tokens, lengths):
        n_steps = tokens.shape[1]
        emis_all = jnp.transpose(jnp.take(emit_blk, tokens, axis=1), (2, 1, 0))
        first_raw = init_blk[None, :] * emis_all[0].astype(jnp.float32)
        norm_c = lax.psum(jnp.sum(first_raw, axis=1), vec_axes)
        alpha_init = first_raw / norm_c[:, None]
        loglik_init = jnp.log(norm_c)

        def one_step(state_in, inputs):
            alpha_cur, loglik = state_in
            emis_t, t_index = inputs
            gathered = lax.all_gather(alpha_cur.astype(jnp.bfloat16), 'states', axis=1, tiled=True)
            part_sum = jnp.einsum('bk,kaq->baq', gathered, trans_blk, preferred_element_type=jnp.float32)
            mix_sum = lax.psum_scatter(part_sum, 'rows', scatter_dimension=1, tiled=True)[:, 0, :]
            raw_next = mix_sum * emis_t.astype(jnp.float32)
            norm_step = lax.psum(jnp.sum(raw_next, axis=1), vec_axes)
            active = t_index < lengths
            alpha_cur = jnp.where(active[:, None], raw_next / norm_step[:, None], alpha_cur)
            loglik = loglik + jnp.where(active, jnp.log(norm_step), 0.0)
            return (alpha_cur, loglik), None

        scan_out = lax.scan(one_step, (alpha_init, loglik_init), (emis_all[1:], jnp.arange(1, n_steps)))
        alpha_last, loglik = scan_out[0]
        return loglik, alpha_last

    return jax.shard_map(local_forward, mesh=mesh, in_specs=(P('rows', None, 'states'), P(vec_axes, None), P(vec_axes), P('seqs', None), P('seqs')), out_specs=(P('seqs'), P('seqs', vec_axes)), check_vma=False)
```

profile of v0, /device:TPU:0, one launch (start us, length us, event | category | flops | bytes accessed | tf_op | source)
XLA Modules:
  0.0 191.0 jit_solution(200740726881587513)
XLA Ops:
  7.2 0.7 compare_select_fusion
  7.9 0.1 reshape.23
  8.1 2.8 %gather_fusion = bf16[256,512]{1,0:T(8,128)(2,1)S(1)} fusion(bf16[512,50257]{0,1:T(8,128)(2,1)} %param.8, s32[1024]{0:T(1024)S(1)} %pad_clamp_fusion), kind=kCustom, calls=%fused_computation | custom fusion | bytes 525312 | tf_op jit(solution)/shard_map/jit(_take)/gather | solution.py:12
  11.1 0.1 fusion.4
  11.2 25.1 %psum.14 = f32[64]{0:T(128)S(1)} all-reduce(f32[64]{0:T(128)S(1)} %fusion.4), channel_id=1, replica_groups=mesh['seqs'=1,'rows'=2,'states'=4] {'rows','states'}, use_global_device_ids=true, to_apply=%region_1.2 | all-reduce | flops 64 | bytes 512 | tf_op jit(solution)/shard_map/psum | solution.py:14
  36.4 4.8 %copy.11 = bf16[2048,2,512]{2,0,1:T(8,128)(2,1)} copy(bf16[2048,2,512]{2,1,0:T(2,128)(2,1)} %param.7) | data formatting | bytes 8388608 | tf_op jit(solution)/shard_map/while | solution.py:31
  41.2 142.5 %while.12 = (s32[]{:T(128)}, f32[64,512]{1,0:T(8,128)S(1)}, f32[64]{0:T(128)S(1)}, s32[3]{0:T(128)S(1)}, s32[64]{0:T(128)S(1)}, /*index=5*/bf16[2048,2,512]{2,0,...) while((s32[]{:T(128)}, f32[64,512]{1,0:T(8,128)S(1)}, f32[64]{0:T(128)S(1)}, s32[3]{0:T(128)S(1)}, ...), condition=%wide.region_6.7_spmd, body=%wide.region_2.6_spmd.sunk | while | flops 268697792 | bytes 7080221 | solution.py:31
  41.3 9.7 %all_gather.4 = bf16[64,2048]{1,0:T(8,128)(2,1)S(1)} all-gather(bf16[64,512]{1,0:T(8,128)(2,1)S(1)} %convert_element_type.20), channel_id=1, replica_groups=mesh['seqs'=1,'rows'=2,'states'=4] {'states'}, dimensions={1}, use_global_device_ids=true | all-gather | bytes 327680 | tf_op jit(solution)/shard_map/while/body/eval_jaxpr/all_gather | solution.py:21
  51.0 3.7 %fusion.12 = f32[64,2,512]{2,0,1:T(8,128)} fusion(bf16[2048,2,512]{2,0,1:T(8,128)(2,1)} %get-tuple-element.140, bf16[64,2048]{1,0:T(8,128)(2,1)S(1)} %all_gather.4), kind=kOutput, calls=%fused_computation.1.clone.1 | convolution fusion | flops 268435456 | bytes 4718592 | tf_op jit(solution)/shard_map/while/body/eval_jaxpr/bk,kaq->baq/dot_general | solution.py:22
  54.7 0.6 dynamic_slice.15
  55.3 8.4 %reduce-scatter.2.cloned.1.call-done = f32[64,1,512]{2,0,1:T(8,128)} async-done(((f32[64,2,512]{2,0,1:T(8,128)}), f32[64,1,512]{2,0,1:T(8,128)}) %reduce-scatter.2.cloned.1.call-update) | async-done | bytes 131088 | tf_op jit(solution)/shard_map/while/body/eval_jaxpr/reduce_scatter | solution.py:23
  63.8 1.0 fusion.13
  64.8 22.2 %psum.16 = f32[64]{0:T(128)S(1)} all-reduce(f32[64]{0:T(128)S(1)} %fusion.13), channel_id=1, replica_groups=mesh['seqs'=1,'rows'=2,'states'=4] {'rows','states'}, use_global_device_ids=true, to_apply=%region_5.5 | all-reduce | flops 64 | bytes 512 | tf_op jit(solution)/shard_map/while/body/eval_jaxpr/psum | solution.py:25
  87.1 0.7 select_add_fusion.2
  87.7 1.0 divide_select_fusion.2
  88.8 9.7 %all_gather.4 = bf16[64,2048]{1,0:T(8,128)(2,1)S(1)} all-gather(bf16[64,512]{1,0:T(8,128)(2,1)S(1)} %convert_element_type.20), channel_id=1, replica_groups=mesh['seqs'=1,'rows'=2,'states'=4] {'states'}, dimensions={1}, use_global_device_ids=true | all-gather | bytes 327680 | tf_op jit(solution)/shard_map/while/body/eval_jaxpr/all_gather | solution.py:21
  98.5 3.7 %fusion.12 = f32[64,2,512]{2,0,1:T(8,128)} fusion(bf16[2048,2,512]{2,0,1:T(8,128)(2,1)} %get-tuple-element.140, bf16[64,2048]{1,0:T(8,128)(2,1)S(1)} %all_gather.4), kind=kOutput, calls=%fused_computation.1.clone.1 | convolution fusion | flops 268435456 | bytes 4718592 | tf_op jit(solution)/shard_map/while/body/eval_jaxpr/bk,kaq->baq/dot_general | solution.py:22
  102.3 0.6 dynamic_slice.15
  102.8 8.4 %reduce-scatter.2.cloned.1.call-done = f32[64,1,512]{2,0,1:T(8,128)} async-done(((f32[64,2,512]{2,0,1:T(8,128)}), f32[64,1,512]{2,0,1:T(8,128)}) %reduce-scatter.2.cloned.1.call-update) | async-done | bytes 131088 | tf_op jit(solution)/shard_map/while/body/eval_jaxpr/reduce_scatter | solution.py:23
  111.3 1.0 fusion.13
  112.3 22.3 %psum.16 = f32[64]{0:T(128)S(1)} all-reduce(f32[64]{0:T(128)S(1)} %fusion.13), channel_id=1, replica_groups=mesh['seqs'=1,'rows'=2,'states'=4] {'rows','states'}, use_global_device_ids=true, to_apply=%region_5.5 | all-reduce | flops 64 | bytes 512 | tf_op jit(solution)/shard_map/while/body/eval_jaxpr/psum | solution.py:25
  134.6 0.7 select_add_fusion.2
  135.2 1.0 divide_select_fusion.2
  136.3 9.7 %all_gather.4 = bf16[64,2048]{1,0:T(8,128)(2,1)S(1)} all-gather(bf16[64,512]{1,0:T(8,128)(2,1)S(1)} %convert_element_type.20), channel_id=1, replica_groups=mesh['seqs'=1,'rows'=2,'states'=4] {'states'}, dimensions={1}, use_global_device_ids=true | all-gather | bytes 327680 | tf_op jit(solution)/shard_map/while/body/eval_jaxpr/all_gather | solution.py:21
  146.1 3.7 %fusion.12 = f32[64,2,512]{2,0,1:T(8,128)} fusion(bf16[2048,2,512]{2,0,1:T(8,128)(2,1)} %get-tuple-element.140, bf16[64,2048]{1,0:T(8,128)(2,1)S(1)} %all_gather.4), kind=kOutput, calls=%fused_computation.1.clone.1 | convolution fusion | flops 268435456 | bytes 4718592 | tf_op jit(solution)/shard_map/while/body/eval_jaxpr/bk,kaq->baq/dot_general | solution.py:22
  149.8 0.6 dynamic_slice.15
  150.4 8.5 %reduce-scatter.2.cloned.1.call-done = f32[64,1,512]{2,0,1:T(8,128)} async-done(((f32[64,2,512]{2,0,1:T(8,128)}), f32[64,1,512]{2,0,1:T(8,128)}) %reduce-scatter.2.cloned.1.call-update) | async-done | bytes 131088 | tf_op jit(solution)/shard_map/while/body/eval_jaxpr/reduce_scatter | solution.py:23
  158.8 1.0 fusion.13
  159.9 22.2 %psum.16 = f32[64]{0:T(128)S(1)} all-reduce(f32[64]{0:T(128)S(1)} %fusion.13), channel_id=1, replica_groups=mesh['seqs'=1,'rows'=2,'states'=4] {'rows','states'}, use_global_device_ids=true, to_apply=%region_5.5 | all-reduce | flops 64 | bytes 512 | tf_op jit(solution)/shard_map/while/body/eval_jaxpr/psum | solution.py:25
  182.1 0.7 select_add_fusion.2
  182.8 1.0 divide_select_fusion.2
  183.8 0.6 copy-done
  (27 shorter events, 0.6 us)
Async XLA Ops:
  8.1 2.9 %copy-start.4 = (s32[64,4]{0,1:T(4,128)S(1)}, s32[64,4]{0,1:T(4,128)}, u32[]{:S(2)}) copy-start(s32[64,4]{0,1:T(4,128)} %param.10) | copy-start | bytes 3076
  8.1 3.0 %copy-start.3 = (f32[512]{0:T(512)S(1)}, f32[512]{0:T(512)}, u32[]{:S(2)}) copy-start(f32[512]{0:T(512)} %param.9) | copy-start | bytes 6148
  36.4 4.8 %copy-start.1 = (s32[64]{0:T(128)S(1)}, s32[64]{0:T(128)}, u32[]{:S(2)}) copy-start(s32[64]{0:T(128)} %param.11) | copy-start | bytes 772
  41.2 22.5 %reduce-scatter.2.cloned.1.call-start = ((), (), s32[]{:S(2)}) async-start(), calls=%async_computation.1 | async-start | bytes 393216 | tf_op jit(solution)/shard_map/while/body/eval_jaxpr/reduce_scatter | solution.py:23
  88.7 22.6 %reduce-scatter.2.cloned.1.call-start = ((), (), s32[]{:S(2)}) async-start(), calls=%async_computation.1 | async-start | bytes 393216 | tf_op jit(solution)/shard_map/while/body/eval_jaxpr/reduce_scatter | solution.py:23
  136.2 22.6 %reduce-scatter.2.cloned.1.call-start = ((), (), s32[]{:S(2)}) async-start(), calls=%async_computation.1 | async-start | bytes 393216 | tf_op jit(solution)/shard_map/while/body/eval_jaxpr/reduce_scatter | solution.py:23
  183.8 0.7 copy-start
  183.8 0.6 copy-start.2
Sparse Core Ops, SparseCore 0:
  54.9 8.8 reduce-scatter.1
  102.4 8.8 reduce-scatter.1
  149.9 8.8 reduce-scatter.1
where the time goes:
time: 192 us; the launch traced here: 191 us
  blocking collectives  121 us (63%)
  waiting for transfers between devices  25.4 us (13%)
  between operations  13.8 us (7%)
  matrix products  11.1 us (6%)
  local copies, waits for them, and re-layouts  10.3 us (5%)
  other arithmetic  9.08 us (5%)
    psum x3, blocking collectives, one_step(): norm_step = lax.psum(jnp.sum(raw_next, axis=1), vec_axes)  66.7 us
    all_gather x3, blocking collectives, one_step(): lax.all_gather(alpha_cur.astype(jnp.bfloat16), 'states', axis=1, tiled=True)  29.2 us
    reduce_scatter x3, waiting for transfers between devices, one_step(): lax.psum_scatter(part_sum, 'rows', scatter_dimension=1, tiled=True)[:, 0, :]  25.4 us
    psum x1, blocking collectives, local_forward(): norm_c = lax.psum(jnp.sum(first_raw, axis=1), vec_axes)  25.1 us
    dot_general x3, matrix products, one_step(): jnp.einsum('bk,kaq->baq', gathered, trans_blk, preferred_element_type=jnp...  11.1 us
    while x1, local copies, waits for them, and re-layouts, local_forward(): lax.scan(one_step, (alpha_init, loglik_init), (emis_all[1:], jnp.arange(1...  4.79 us
  transfers between devices with their start and end apart: 3, of which 3 were waited for; matrix products, arithmetic and copies ran while one was open for 1% of the time, Pallas kernels for 0%

commit v1 on v0

v1 whole, which is shorter than its diff:
```python
import functools

import jax
import jax.numpy as jnp
from jax import lax
from jax.experimental import pallas as pl
from jax.experimental.pallas import tpu as pltpu
from jax.sharding import PartitionSpec as P

MESH = pl.DeviceIdType.MESH
F32, BF16 = jnp.float32, jnp.bfloat16
LANES, SUBL = 128, 8


def fold_rows(col, groups):
    lane = lax.broadcasted_iota(jnp.int32, (SUBL, LANES), 1)
    out = jnp.zeros((SUBL, LANES), F32)
    for g in range(groups):
        out = jnp.where(lane == g, col[g * SUBL:(g + 1) * SUBL], out)
    return out


def spread_rows(folded, groups):
    return jnp.concatenate([folded[:, g:g + 1] for g in range(groups)], axis=0)


def interleave(block, out_ref):
    rows, cols = block.shape
    x = block.astype(F32)
    lane = lax.broadcasted_iota(jnp.int32, (rows, LANES), 1)
    for j in range(cols // LANES):
        xj = x[:, j * LANES:(j + 1) * LANES]
        for h in range(2):
            g = jnp.take_along_axis(xj, lane // 2 + h * (LANES // 2), axis=1)
            c0 = (2 * j + h) * LANES
            out_ref[0:rows, c0:c0 + LANES] = jnp.where(lane % 2 == 0, g, 0.0).astype(BF16)
            out_ref[rows:2 * rows, c0:c0 + LANES] = jnp.where(lane % 2 == 1, g, 0.0).astype(BF16)


def kernel(n_steps, len_ref, emis_ref, init_ref, trans_hbm, ll_ref, alpha_ref,
           trans, emis_row, init_row, emis_col, c_out, c_in, part, u_in, a_out, a_in, left,
           load_sem, s_sem, r_sem):
    batch, q = alpha_ref.shape
    groups = batch // SUBL
    z = lax.axis_index('seqs')
    i = lax.axis_index('rows')
    s = lax.axis_index('states')
    x, c = s // 2, s % 2

    def peer(d):
        dy, dx, dc = d // 4, (d // 2) % 2, d % 2
        return (z, 1 - i if dy else i, 2 * (1 - x if dx else x) + (1 - c if dc else c))

    load = pltpu.make_async_copy(trans_hbm.reshape(trans.shape), trans, load_sem)
    load.start()

    barrier = pltpu.get_barrier_semaphore()
    for d in range(1, 8):
        pl.semaphore_signal(barrier, inc=1, device_id=peer(d), device_id_type=MESH)
    pl.semaphore_wait(barrier, 7)

    sent = []

    def send(src, dst, d):
        k = len(sent)
        cp = pltpu.make_async_remote_copy(src_ref=src, dst_ref=dst, send_sem=s_sem.at[k], recv_sem=r_sem.at[k], device_id=peer(d), device_id_type=MESH)
        cp.start()
        sent.append(cp)
        return cp

    def send_c(t, partial):
        c_out[t] = fold_rows(jnp.sum(partial, axis=1, keepdims=True), groups)
        return [send(c_out.at[t], c_in.at[t, d - 1], d) for d in range(1, 8)]

    def recv_c(t, copies):
        for cp in copies:
            cp.wait_recv()
        total = c_out[t]
        for d in range(1, 8):
            total = total + c_in[t, d - 1]
        return total

    def lane_sum(v):
        out = v[:, 0:LANES]
        for j in range(1, q // LANES):
            out = out + v[:, j * LANES:(j + 1) * LANES]
        return out

    copies_e = [send(emis_ref.at[0], emis_row.at[d - 1], d) for d in (1, 2, 3)]
    copies_p = [send(init_ref, init_row.at[d - 1], d) for d in (1, 2, 3)]
    raw = init_ref[...] * emis_ref[0].astype(F32)
    copies_c = send_c(0, lane_sum(raw))
    copies_ep = [send(emis_ref.at[t], emis_col.at[t - 1], 4) for t in range(1, n_steps)]

    sub = lax.broadcasted_iota(jnp.int32, (SUBL, LANES), 0)
    lane = lax.broadcasted_iota(jnp.int32, (SUBL, LANES), 1)
    lens = jnp.zeros((SUBL, LANES), jnp.int32)
    for b in range(batch):
        lens = jnp.where((sub == b % SUBL) & (lane == b // SUBL), len_ref[b], lens)

    c_tot = recv_c(0, copies_c)
    ll = jnp.log(c_tot)
    c_col = spread_rows(c_tot, groups)
    alpha = raw / c_col
    alpha_ref[...] = alpha
    interleave(alpha.astype(BF16), left.at[0])
    for d in (1, 2, 3):
        copies_e[d - 1].wait_recv()
        copies_p[d - 1].wait_recv()
        blk = (init_row[d - 1] * emis_row[d - 1].astype(F32)) / c_col
        interleave(blk.astype(BF16), left.at[d])
    load.wait()

    for t in range(1, n_steps):
        acc = None
        for d in range(4):
            if t > 1 and d > 0:
                copies_a[d - 1].wait_recv()
                interleave(a_in[t - 2, d - 1], left.at[d])
            sp = peer(d)[2]
            rows = pl.ds(pl.multiple_of(sp * 2 * q, 2 * q), 2 * q)
            prod = jnp.dot(left[d], trans[rows, :], preferred_element_type=F32)
            acc = prod if acc is None else acc + prod
        part[t - 1] = acc
        mine = pl.ds(pl.multiple_of(i * batch, batch), batch)
        other = pl.ds(pl.multiple_of((1 - i) * batch, batch), batch)
        copy_u = send(part.at[t - 1, other], u_in.at[t - 1], 4)
        emis_t = emis_ref[t].astype(F32)
        copies_ep[t - 1].wait_recv()
        own = part[t - 1, mine]
        w = own * emis_t + part[t - 1, other] * emis_col[t - 1].astype(F32)
        copies_c = send_c(t, lane_sum(w))
        copy_u.wait_recv()
        raw = (own + u_in[t - 1]) * emis_t
        c_tot = recv_c(t, copies_c)
        active = lens > t
        ll = ll + jnp.where(active, jnp.log(c_tot), 0.0)
        c_col = spread_rows(c_tot, groups)
        act_col = spread_rows(active.astype(F32), groups)
        alpha = jnp.where(act_col > 0.5, raw / c_col, alpha_ref[...])
        alpha_ref[...] = alpha
        if t < n_steps - 1:
            a_out[t - 1] = alpha.astype(BF16)
            copies_a = [send(a_out.at[t - 1], a_in.at[t - 1, d - 1], d) for d in (1, 2, 3)]
            interleave(alpha.astype(BF16), left.at[0])

    ll = jnp.where(lane < groups, ll, 0.0)
    wide = jnp.take_along_axis(ll, lane // SUBL, axis=1)
    ll_ref[...] = jnp.sum(jnp.where(lane % SUBL == sub, wide, 0.0), axis=0, keepdims=True)[:, :batch]
    for cp in sent:
        cp.wait_send()


def solution(mesh):
    vec_axes = ('rows', 'states')

    def local_forward(trans_blk, emit_blk, init_blk, tokens, lengths):
        batch, n_steps = tokens.shape
        src, two, q = trans_blk.shape
        toks = tokens.T.reshape(-1)
        emis = jnp.take(emit_blk.T, toks, axis=0, mode='clip').reshape(n_steps, batch, q)
        n_copies = 3 + 3 + 7 * n_steps + (n_steps - 1) * 2 + 3 * (n_steps - 2)
        vmem = pl.BlockSpec(memory_space=pltpu.VMEM)
        ll, alpha = pl.pallas_call(
            functools.partial(kernel, n_steps),
            out_shape=(jax.ShapeDtypeStruct((1, batch), F32), jax.ShapeDtypeStruct((batch, q), F32)),
            in_specs=[pl.BlockSpec(memory_space=pltpu.SMEM), vmem, vmem, pl.BlockSpec(memory_space=pl.ANY)],
            out_specs=(vmem, vmem),
            scratch_shapes=[
                pltpu.VMEM((2 * src, q), BF16),
                pltpu.VMEM((3, batch, q), BF16),
                pltpu.VMEM((3, 1, q), F32),
                pltpu.VMEM((n_steps - 1, batch, q), BF16),
                pltpu.VMEM((n_steps, SUBL, LANES), F32),
                pltpu.VMEM((n_steps, 7, SUBL, LANES), F32),
                pltpu.VMEM((n_steps - 1, 2 * batch, q), F32),
                pltpu.VMEM((n_steps - 1, batch, q), F32),
                pltpu.VMEM((n_steps - 2, batch, q), BF16),
                pltpu.VMEM((n_steps - 2, 3, batch, q), BF16),
                pltpu.VMEM((4, 2 * batch, 2 * q), BF16),
                pltpu.SemaphoreType.DMA,
                pltpu.SemaphoreType.DMA((n_copies,)),
                pltpu.SemaphoreType.DMA((n_copies,)),
            ],
            compiler_params=pltpu.CompilerParams(collective_id=0, has_side_effects=True),
        )(lengths, emis, init_blk.reshape(1, q), trans_blk)
        return ll.reshape(batch), alpha

    return jax.shard_map(local_forward, mesh=mesh, in_specs=(P('rows', None, 'states'), P(vec_axes, None), P(vec_axes), P('seqs', None), P('seqs')), out_specs=(P('seqs'), P('seqs', vec_axes)), check_vma=False)
```

time: 192 us -> 46.8 us (0.24)
  blocking collectives: 121 us -> 0 us
  Pallas kernels: 0 us -> 39 us
  waiting for transfers between devices: 25.4 us -> 0 us
  between operations: 13.8 us -> 0.64 us
  matrix products: 11.1 us -> 0 us
  other arithmetic: 9.08 us -> 0.01 us
  local copies, waits for them, and re-layouts: 10.3 us -> 6.94 us
    psum x4 -> x0, blocking collectives: 91.8 us -> none  [the longest x3 66.7 us: one_step(): norm_step = lax.psum(jnp.sum(raw_next, axis=1), vec_axes)]
    pallas_call x0 -> x1, Pallas kernels: none -> 39 us  [local_forward(): pl.pallas_call(functools.partial(kernel, n_steps), out_shape=(jax.ShapeDt...]
    all_gather x3 -> x0, blocking collectives: 29.2 us -> none  [one_step(): lax.all_gather(alpha_cur.astype(jnp.bfloat16), 'states', axis=1, tiled=True)]
    reduce_scatter x3 -> x0, waiting for transfers between devices: 25.4 us -> none  [one_step(): lax.psum_scatter(part_sum, 'rows', scatter_dimension=1, tiled=True)[:, 0, :]]
    dot_general x3 -> x0, matrix products: 11.1 us -> none  [one_step(): jnp.einsum('bk,kaq->baq', gathered, trans_blk, preferred_element_type=jnp...]
    while x1 -> x0, local copies, waits for them, and re-layouts: 4.79 us -> none  [local_forward(): lax.scan(one_step, (alpha_init, loglik_init), (emis_all[1:], jnp.arange(1...]
    select_n x5 -> x0, other arithmetic: 3.79 us -> none  [the longest x3 3 us: one_step(): jnp.where(active[:, None], raw_next / norm_step[:, None], alpha_cur)]
    reduce_sum x4 -> x0, other arithmetic: 3.17 us -> none  [the longest x3 3.06 us: one_step(): norm_step = lax.psum(jnp.sum(raw_next, axis=1), vec_axes)]
  transfers between devices with their start and end apart: 3 -> 0, of which waited for: 3 -> 0; matrix products, arithmetic and copies ran while one was open for 1% -> 0% of each run, Pallas kernels for 0% -> 0%
where the time goes in v1:
time: 46.8 us; the launch traced here: 46.6 us
  Pallas kernels  39 us (83%)
  local copies, waits for them, and re-layouts  6.94 us (15%)
  between operations  0.64 us (1%)
    pallas_call x1, Pallas kernels, local_forward(): pl.pallas_call(functools.partial(kernel, n_steps), out_shape=(jax.ShapeDt...  39 us
    gather x1, local copies, waits for them, and re-layouts, local_forward(): jnp.take(emit_blk.T, toks, axis=0, mode='clip').reshape(n_steps, batch, q)  3.49 us
    unnamed x2, local copies, waits for them, and re-layouts  2.69 us

profile of v1, /device:TPU:0, one launch (start us, length us, event | category | flops | bytes accessed | tf_op | source)
XLA Modules:
  0.0 46.6 jit_solution(1030129513010816978)
XLA Ops:
  0.6 0.8 %reshape.20 = s32[256]{0:T(256)S(1)} reshape(s32[4,64]{1,0:T(4,128)} %bitcast.8) | data formatting | bytes 2048 | tf_op jit(solution)/shard_map/jit(_take)/broadcast_in_dim | solution.py:161
  1.4 3.5 %gather_fusion = bf16[256,512]{1,0:T(8,128)(2,1)} fusion(bf16[50257,512]{1,0:T(8,128)(2,1)} %bitcast.6, s32[1024]{0:T(1024)S(1)} %pad_clamp_fusion), kind=kCustom, calls=%fused_computation | custom fusion | bytes 525312 | tf_op jit(solution)/shard_map/jit(_take)/gather | solution.py:161
  4.9 39.0 %shard_map.68 = (f32[1,64]{1,0:T(1,128)}, f32[64,512]{1,0:T(8,128)}) custom-call(s32[64]{0:T(128)} %len_ref.1, bf16[4,64,512]{2,1,0:T(8,128)(2,1)} %bitcast.5, f32[1,512]{1,0:T(1,128)} %bitcast.7, bf16[2048,2,512]{2,1,0:T(2,128)(2,1)} %trans_hbm.1), custom_call_target="tpu_custom_call" | custom-call | tf_op jit(solution)/shard_map/pallas_call | solution.py:164
  43.9 1.1 %copy.9 = f32[64]{0:T(128)} copy(f32[64]{0:T(128)} %bitcast.9) | data formatting | bytes 512
  45.0 1.6 %copy.10 = f32[64,512]{1,0:T(8,128)} copy(f32[64,512]{1,0:T(8,128)} %get-tuple-element.9) | data formatting | bytes 262144
  (1 shorter events, 0.0 us)
